TPU v7x, 32 devices: a whole 2x2x4 slice. The times are simulated.
32 devices in a mesh: time: 8 (over y, x, core), chan: 4 (over z).
Axes of the slice: x: 2, y: 2, z: 4, core: 2. Of those that a mesh axis runs over, the one named last changes fastest.
Arguments:
- decay_rate: float32 [4, 4096, 2560], P(None, 'time', 'chan'), may hold values from 0.2 to 2
- drive_in: bfloat16 [4, 4096, 2560], P(None, 'time', 'chan'), may hold values from -6 to 6
- gate_in: bfloat16 [4, 4096, 2560], P(None, 'time', 'chan'), may hold values from -6 to 6
- norm_gain: float32 [2560], P('chan'), may hold values from 0.25 to 1.75
Outputs:
- filtered: bfloat16 [4, 4096, 2560], P(None, 'time', 'chan')
All inputs are finite; a program needn't handle non-finite values.
Results may differ from a plain program's by a relative error of at most 0.0015.
Values sent between devices are 32-bit elements.
A program may use at most 128 MiB of HBM per device.

v0:
```python
import jax
import jax.numpy as jnp
from jax import lax
from jax.sharding import PartitionSpec as P


def entering(value, axis, join, neutral, backward):
    count, mine = lax.axis_size(axis), lax.axis_index(axis)
    pieces = jax.tree.map(lambda part: lax.all_gather(part, axis), value)
    if backward:
        pieces = jax.tree.map(lambda part: part[::-1], pieces)
        mine = count - 1 - mine
    so_far = jax.tree.map(
        lambda part, zero: jnp.full_like(part, 0) + jnp.asarray(zero, part.dtype), value, neutral
    )

    def turn(position, so_far):
        longer = join(so_far, jax.tree.map(lambda part: part[position], pieces))
        return jax.tree.map(lambda new, old: jnp.where(position < mine, new, old), longer, so_far)

    return lax.fori_loop(0, count - 1, turn, so_far)


def join_pair(earlier, later):
    return (earlier[0] * later[0], later[0] * earlier[1] + later[1])


def shards(decay_rate, drive_in, gate_in, norm_gain):
    total_length = decay_rate.shape[1] * lax.axis_size("time")
    keep = jnp.exp(-decay_rate / total_length)
    push = drive_in.astype(jnp.float32) * total_length ** (-0.5)
    steps = -decay_rate / total_length
    logs = jnp.sum(steps, axis=1, keepdims=True) - jnp.cumsum(steps, axis=1)
    summary = (jnp.exp(jnp.sum(steps, axis=1)), jnp.sum(jnp.exp(logs) * push, axis=1))
    entering_forward = entering(
        summary, "time", join_pair, (jnp.ones_like(keep[:, 0]), jnp.zeros_like(push[:, 0])), False
    )
    started = push.at[:, 0].add(keep[:, 0] * entering_forward[1])
    forward = lax.associative_scan(join_pair, (keep, started), axis=1)[1]
    gated = forward * jax.nn.sigmoid(gate_in.astype(jnp.float32))
    power = lax.psum(jnp.sum(gated * gated, axis=-1, keepdims=True), "chan") / (
        gated.shape[-1] * lax.axis_size("chan")
    )
    filtered = (gated * lax.rsqrt(power + 1e-06) * norm_gain).astype(jnp.bfloat16)
    return filtered


def solution(mesh):
    placed = (P(None, "time", "chan"), P(None, "time", "chan"), P(None, "time", "chan"), P("chan"))
    return jax.shard_map(
        shards, mesh=mesh, in_specs=placed, out_specs=P(None, "time", "chan"), check_vma=False
    )
```

profile of v0, /device:TPU:0, one launch (start us, length us, event | category | flops | bytes accessed | tf_op | source)
XLA Modules:
  0.0 252.6 jit_solution(16648536298817742762)
XLA Ops:
  0.0 7.1 %fusion.17 = (f32[4,512,640]{2,1,0:T(8,128)}, f32[4,640]{1,0:T(4,128)S(1)}, f32[4,512,640]{2,1,0:T(8,128)}) fusion(f32[4,512,640]{2,1,0:T(8,128)} %param.8), kind=kLoop, calls=%fused_computation.61 | loop fusion | flops 3929600 | bytes 15738880 | tf_op jit(solution)/shard_map/exp | solution.py:30
  7.1 8.2 %fusion.3 = f32[4,640,4,128]{1,2,3,0:T(4,128)} fusion(f32[4,640,4,128]{1,3,2,0:T(8,128)} %bitcast.49), kind=kOutput, calls=%fused_computation.7 | output fusion | flops 166461440 | bytes 10485760 | tf_op jit(solution)/shard_map/reduce-window
  15.3 0.9 slice.307
  16.2 0.8 slice_bitcast_fusion
  17.1 3.4 %broadcast_add_fusion = f32[4,640,4,128]{1,2,3,0:T(4,128)S(1)} fusion(f32[4,640,4,128]{1,2,3,0:T(4,128)} %fusion.3, f32[4,640,4]{1,2,0:T(4,128)S(1)} %slice.309), kind=kLoop, calls=%fused_computation.18 | loop fusion | flops 1310720 | bytes 10526720 | tf_op jit(solution)/shard_map/reduce_window_sum
  20.5 0.6 copy.18
  21.1 1.1 copy-done.1
  22.2 3.5 %fusion.1 = (f32[4,640]{1,0:T(4,128)S(1)}, f32[4,512,640]{2,1,0:T(8,128)}) fusion(f32[4,640,4,128]{1,3,2,0:T(8,128)S(1)} %copy.18, f32[4,640]{1,0:T(4,128)S(1)} %get-tuple-element.143, bf16[4,512,640]{2,1,0:T(8,128)(2,1)S(1)} %copy-done.1), kind=kLoop, calls=%fused_computation.4 | loop fusion | flops 6551040 | bytes 13127680 | tf_op jit(solution)/shard_map/reduce_sum | solution.py:34
  25.8 10.7 %all-gather.3 = f32[8,4,640]{2,1,0:T(4,128)S(1)} all-gather(f32[1,4,640]{2,1,0:T(4,128)S(1)} %bitcast.64), channel_id=3, replica_groups=mesh['time'=8,'chan'=4] {'time'}, dimensions={0}, use_global_device_ids=true | all-gather | bytes 92160 | tf_op jit(solution)/shard_map/all_gather | solution.py:9
  36.4 9.3 %all-gather.2 = f32[8,4,640]{2,1,0:T(4,128)S(1)} all-gather(f32[1,4,640]{2,1,0:T(4,128)S(1)} %exponential_bitcast_fusion), channel_id=2, replica_groups=mesh['time'=8,'chan'=4] {'time'}, dimensions={0}, use_global_device_ids=true | all-gather | bytes 92160 | tf_op jit(solution)/shard_map/all_gather | solution.py:9
  45.8 0.3 while.15
  46.1 0.9 slice_add_fusion.2
  47.0 1.6 scatter-add.4
  48.5 14.1 %slice.305 = f32[4,255,640]{2,1,0:T(8,128)} slice(f32[4,512,640]{2,1,0:T(8,128)} %scatter-add.4), slice={[0:4:1], [2:512:2], [0:640:1]} | slice | bytes 5222400 | tf_op jit(solution)/shard_map/slice | solution.py:39
  62.6 14.0 %slice.243 = f32[4,256,640]{2,1,0:T(8,128)} slice(f32[4,512,640]{2,1,0:T(8,128)} %scatter-add.4), slice={[0:4:1], [1:512:2], [0:640:1]} | slice | bytes 5242880 | tf_op jit(solution)/shard_map/slice | solution.py:39
  76.6 14.0 %slice.242 = f32[4,256,640]{2,1,0:T(8,128)} slice(f32[4,512,640]{2,1,0:T(8,128)} %scatter-add.4), slice={[0:4:1], [0:511:2], [0:640:1]} | slice | bytes 5242880 | tf_op jit(solution)/shard_map/slice | solution.py:39
  90.6 14.0 %slice.245 = f32[4,256,640]{2,1,0:T(8,128)} slice(f32[4,512,640]{2,1,0:T(8,128)} %get-tuple-element.142), slice={[0:4:1], [0:511:2], [0:640:1]} | slice | bytes 5242880 | tf_op jit(solution)/shard_map/slice | solution.py:39
  104.6 13.9 %slice.241 = f32[4,256,640]{2,1,0:T(8,128)} slice(f32[4,512,640]{2,1,0:T(8,128)} %get-tuple-element.142), slice={[0:4:1], [1:512:2], [0:640:1]} | slice | bytes 5242880 | tf_op jit(solution)/shard_map/slice | solution.py:39
  118.5 6.1 %fusion.18 = (f32[4,256,640]{2,1,0:T(8,128)}, f32[4,256,640]{2,1,0:T(8,128)S(1)}) fusion(f32[4,256,640]{2,1,0:T(8,128)} %slice.245, f32[4,256,640]{2,1,0:T(8,128)} %slice.241, f32[4,256,640]{2,1,0:T(8,128)} %slice.243, f32[4,256,640]{2,1,0:T(8,128)} %slice.242), kind=kLoop, calls=%fused_computation.62 | loop fusion | flops 1966080 | bytes 15728640 | tf_op jit(solution)/shard_map/mul | solution.py:25
  124.7 14.1 %slice.240 = f32[4,255,640]{2,1,0:T(8,128)} slice(f32[4,512,640]{2,1,0:T(8,128)} %get-tuple-element.142), slice={[0:4:1], [2:512:2], [0:640:1]} | slice | bytes 5222400 | tf_op jit(solution)/shard_map/slice | solution.py:39
  138.7 7.5 %slice.251 = f32[4,128,640]{2,1,0:T(8,128)} slice(f32[4,256,640]{2,1,0:T(8,128)} %get-tuple-element.145), slice={[0:4:1], [0:255:2], [0:640:1]} | slice | bytes 2621440 | tf_op jit(solution)/shard_map/slice | solution.py:39
  146.2 7.5 %slice.247 = f32[4,128,640]{2,1,0:T(8,128)} slice(f32[4,256,640]{2,1,0:T(8,128)} %get-tuple-element.145), slice={[0:4:1], [1:256:2], [0:640:1]} | slice | bytes 2621440 | tf_op jit(solution)/shard_map/slice | solution.py:39
  153.7 7.5 %slice.246 = f32[4,127,640]{2,1,0:T(8,128)} slice(f32[4,256,640]{2,1,0:T(8,128)} %get-tuple-element.145), slice={[0:4:1], [2:256:2], [0:640:1]} | slice | bytes 2600960 | tf_op jit(solution)/shard_map/slice | solution.py:39
  161.3 4.4 %slice.303 = f32[4,127,640]{2,1,0:T(8,128)} slice(f32[4,256,640]{2,1,0:T(8,128)S(1)} %get-tuple-element.146), slice={[0:4:1], [2:256:2], [0:640:1]} | slice | bytes 2600960 | tf_op jit(solution)/shard_map/slice | solution.py:39
  165.6 4.3 %slice.249 = f32[4,128,640]{2,1,0:T(8,128)} slice(f32[4,256,640]{2,1,0:T(8,128)S(1)} %get-tuple-element.146), slice={[0:4:1], [1:256:2], [0:640:1]} | slice | bytes 2621440 | tf_op jit(solution)/shard_map/slice | solution.py:39
  169.9 4.2 %slice.248 = f32[4,128,640]{2,1,0:T(8,128)} slice(f32[4,256,640]{2,1,0:T(8,128)S(1)} %get-tuple-element.146), slice={[0:4:1], [0:255:2], [0:640:1]} | slice | bytes 2621440 | tf_op jit(solution)/shard_map/slice | solution.py:39
  174.1 2.8 %fusion.19 = (f32[4,128,640]{2,1,0:T(8,128)S(1)}, f32[4,128,640]{2,1,0:T(8,128)S(1)}) fusion(f32[4,128,640]{2,1,0:T(8,128)} %slice.251, f32[4,128,640]{2,1,0:T(8,128)} %slice.247, f32[4,128,640]{2,1,0:T(8,128)} %slice.249, f32[4,128,640]{2,1,0:T(8,128)} %slice.248), kind=kLoop, calls=%fused_computation.63 | loop fusion | flops 983040 | bytes 7864320 | tf_op jit(solution)/shard_map/mul | solution.py:25
  176.9 1.6 slice.257
  178.5 1.5 slice.253
  180.0 0.4 slice.252
  180.4 0.5 slice.301
  180.9 1.5 slice.255
  182.4 1.5 slice.254
  184.0 1.6 fusion.20
  185.6 0.8 slice.263
  186.5 0.8 slice.259
  187.3 0.8 slice.258
  188.1 0.2 slice.299
  188.3 0.2 slice.261
  188.5 0.8 slice.260
  189.3 1.2 fusion.21
  190.5 0.1 slice.269
  190.6 0.1 slice.265
  190.8 0.1 slice.264
  190.9 0.1 slice.297
  191.1 0.1 slice.267
  193.2 0.2 pad.67
  193.3 0.2 pad.68
  193.5 0.1 fusion.7
  193.8 0.3 pad.69
  194.0 0.3 pad.70
  194.3 2.0 fusion.6
  196.3 1.2 add.183
  197.5 1.2 pad_maximum_fusion.1
  198.7 2.4 pad.71
  201.1 5.3 %pad.72 = f32[4,256,640]{2,1,0:T(8,128)} pad(f32[4,128,640]{2,1,0:T(8,128)} %add.183, f32[]{:T(128)} %constant.68.clone.1), padding=0_0_0x1_0_1x0_0_0 | pad | bytes 3932164 | tf_op jit(solution)/shard_map/pad | solution.py:39
  206.4 3.9 %fusion.5 = f32[4,255,640]{2,1,0:T(8,128)S(1)} fusion(f32[4,255,640]{2,1,0:T(8,128)} %slice.305, f32[4,255,640]{2,1,0:T(8,128)} %slice.240, f32[4,256,640]{2,1,0:T(8,128)} %pad.72, f32[4,256,640]{2,1,0:T(8,128)S(1)} %pad.71), kind=kLoop, calls=%fused_computation.15 | loop fusion | flops 1958400 | bytes 13056000 | tf_op jit(solution)/shard_map/add | solution.py:25
  210.5 1.9 add.185
  212.4 0.2 pad_maximum_fusion
  212.6 6.6 %pad.73 = f32[4,512,640]{2,1,0:T(8,128)} pad(f32[4,256,640]{2,1,0:T(8,128)S(1)} %pad_maximum_fusion, f32[]{:T(128)} %constant.68.clone.1), padding=0_0_0x0_1_1x0_0_0 | pad | bytes 7864324 | tf_op jit(solution)/shard_map/pad | solution.py:39
  219.2 10.3 %pad.74 = f32[4,512,640]{2,1,0:T(8,128)} pad(f32[4,256,640]{2,1,0:T(8,128)} %add.185, f32[]{:T(128)} %constant.68.clone.1), padding=0_0_0x1_0_1x0_0_0 | pad | bytes 7864324 | tf_op jit(solution)/shard_map/pad | solution.py:39
  229.5 6.4 %multiply_reduce_fusion = (f32[4,512]{1,0:T(4,128)S(1)}, f32[4,512,640]{2,1,0:T(8,128)}) fusion(bf16[4,512,640]{2,1,0:T(8,128)(2,1)S(1)} %copy-done.3, f32[4,512,640]{2,1,0:T(8,128)} %pad.73, f32[4,512,640]{2,1,0:T(8,128)} %pad.74), kind=kLoop, calls=%fused_computation.10 | loop fusion | flops 10483712 | bytes 18358272 | tf_op jit(solution)/shard_map/reduce_sum | solution.py:41
  235.9 12.1 %psum.7 = f32[4,512,1]{1,0,2:T(4,128)S(1)} all-reduce(f32[4,512,1]{1,0,2:T(4,128)S(1)} %bitcast.65), channel_id=1, replica_groups=mesh['time'=8,'chan'=4] {'chan'}, use_global_device_ids=true, to_apply=%region_7.8 | all-reduce | flops 2048 | bytes 16384 | tf_op jit(solution)/shard_map/psum | solution.py:41
  248.0 4.5 %multiply_convert_fusion = bf16[4,512,640]{2,1,0:T(8,128)(2,1)} fusion(f32[4,512,640]{2,1,0:T(8,128)} %get-tuple-element.141, f32[640]{0:T(1024)S(1)} %copy-done.5, f32[4,512]{1,0:T(4,128)S(1)} %rsqrt_bitcast_fusion), kind=kLoop, calls=%fused_computation.9 | loop fusion | flops 3932160 | bytes 7875072 | tf_op jit(solution)/shard_map/convert_element_type | solution.py:44
  (77 shorter events, 2.2 us)
Async XLA Ops:
  20.5 1.7 copy-start.1
  180.4 3.6 %copy-start.2 = (f32[4,64,640]{2,1,0:T(8,128)S(1)}, f32[4,64,640]{2,1,0:T(8,128)}, u32[]{:S(2)}) copy-start(f32[4,64,640]{2,1,0:T(8,128)} %slice.257) | copy-start | bytes 1966084
  191.9 1.1 copy-start.4
  206.4 4.0 %copy-start = (f32[4,256,640]{2,1,0:T(8,128)S(1)}, f32[4,256,640]{2,1,0:T(8,128)}, u32[]{:S(2)}) copy-start(f32[4,256,640]{2,1,0:T(8,128)} %pad.72) | copy-start | bytes 7864324
  219.2 10.3 %copy-start.3 = (bf16[4,512,640]{2,1,0:T(8,128)(2,1)S(1)}, bf16[4,512,640]{2,1,0:T(8,128)(2,1)}, u32[]{:S(2)}) copy-start(bf16[4,512,640]{2,1,0:T(8,128)(2,1)} %param.10) | copy-start | bytes 7864324
  229.5 18.5 %copy-start.5 = (f32[640]{0:T(1024)S(1)}, f32[640]{0:T(1024)}, u32[]{:S(2)}) copy-start(f32[640]{0:T(1024)} %param.11) | copy-start | bytes 7684
where the time goes:
time: 256 us; the launch traced here: 253 us
  local copies, waits for them, and re-layouts  163 us (64%)
  other arithmetic  57.2 us (22%)
  blocking collectives  32.1 us (13%)
    slice x52, local copies, waits for them, and re-layouts, shards(): forward = lax.associative_scan(join_pair, (keep, started), axis=1)[1]  131 us
    pad x16, local copies, waits for them, and re-layouts, shards(): forward = lax.associative_scan(join_pair, (keep, started), axis=1)[1]  26 us
    all_gather x2, blocking collectives, entering(): pieces = jax.tree.map(lambda part: lax.all_gather(part, axis), value)  20 us
    psum x1, blocking collectives, shards(): lax.psum(jnp.sum(gated * gated, axis=-1, keepdims=True), 'chan')  12.1 us
    mul x7, other arithmetic, join_pair(): return (earlier[0] * later[0], later[0] * earlier[1] + later[1])  11.8 us
    another operation x4, other arithmetic  11.7 us
    exp x1, other arithmetic, shards(): keep = jnp.exp(-decay_rate / total_length)  7.07 us
    reduce_sum x1, other arithmetic, shards(): jnp.sum(gated * gated, axis=-1, keepdims=True)  6.4 us

commit v1 on v0

v1 whole, which is shorter than its diff:
```python
import functools
import math

import jax
import jax.numpy as jnp
from jax import lax
from jax.experimental import pallas as pl
from jax.experimental.pallas import tpu as pltpu
from jax.sharding import PartitionSpec as P

BLOCK = 128
LANES = 128
MESH = pl.DeviceIdType.MESH


def split(x):
    hi = x.astype(jnp.bfloat16)
    lo = (x - hi.astype(jnp.float32)).astype(jnp.bfloat16)
    return jnp.concatenate([hi, lo], axis=0)


def kernel(times, chans, dec_hbm, drv_hbm, gate_hbm, gain_ref, tri_ref, out_hbm,
           dec, drv, gate, run, outb, keeps, sums, mine, theirs, power, powers,
           in_sem, out_sem, t_send, t_recv, c_send, c_recv):
    batch, length, width = dec.shape
    blocks = length // BLOCK
    total = length * times
    rate = math.log2(math.e) / total
    scale = 0.5 * total ** -0.5
    t, c = lax.axis_index("time"), lax.axis_index("chan")

    places = ((dec_hbm, dec), (drv_hbm, drv), (gate_hbm, gate))

    def load(i, b):
        return pltpu.make_async_copy(places[i][0].at[b], places[i][1].at[b], in_sem.at[i, b])

    def store(b):
        return pltpu.make_async_copy(outb.at[b], out_hbm.at[b], out_sem.at[b])

    def time_copy(b, peer):
        return pltpu.make_async_remote_copy(
            src_ref=mine.at[b], dst_ref=theirs.at[b, t], send_sem=t_send.at[b, peer],
            recv_sem=t_recv.at[b, t], device_id={"time": peer}, device_id_type=MESH)

    def time_arrival(b, peer):
        return pltpu.make_async_remote_copy(
            src_ref=mine.at[b], dst_ref=theirs.at[b, peer], send_sem=t_send.at[b, peer],
            recv_sem=t_recv.at[b, peer], device_id={"time": peer}, device_id_type=MESH)

    def chan_copy(b, step):
        return pltpu.make_async_remote_copy(
            src_ref=power.at[b], dst_ref=powers.at[b, step - 1], send_sem=c_send.at[b, step - 1],
            recv_sem=c_recv.at[b, step - 1], device_id={"chan": lax.rem(c + step, chans)},
            device_id_type=MESH)

    for b in range(batch):
        load(0, b).start()
        load(1, b).start()
    for b in range(batch):
        load(2, b).start()

    barrier = pltpu.get_barrier_semaphore()
    for step in range(1, times):
        pl.semaphore_signal(barrier, inc=1, device_id={"time": lax.rem(t + step, times)},
                            device_id_type=MESH)
    for step in range(1, chans):
        pl.semaphore_signal(barrier, inc=1, device_id={"chan": lax.rem(c + step, chans)},
                            device_id_type=MESH)

    def rows(k):
        return pl.ds(pl.multiple_of(k * BLOCK, BLOCK), BLOCK)

    def first(b):
        load(0, b).wait()
        load(1, b).wait()

        def block(k, carried):
            kept, state = carried
            at = rows(k)
            so_far = rate * jnp.dot(tri_ref[...], split(dec[b, at, :]),
                                    preferred_element_type=jnp.float32)
            entered = jnp.exp2(so_far) * drv[b, at, :].astype(jnp.float32)
            dec[b, at, :] = so_far
            run[b, at, :] = entered
            keep = jnp.exp2(-so_far[BLOCK - 1:, :])
            gained = jnp.sum(entered, axis=0, keepdims=True)
            keeps[b, k] = keep
            sums[b, k] = gained
            return kept * keep, keep * (state + gained)

        kept, state = lax.fori_loop(
            0, blocks, block, (jnp.ones((1, width), jnp.float32), jnp.zeros((1, width), jnp.float32)))
        mine[b, 0:1, :] = kept
        mine[b, 1:2, :] = state

    def send_times(b):
        def send(peer, _):
            time_copy(b, peer).start()
            return 0
        lax.fori_loop(t + 1, times, send, 0)

    first(0)
    pl.semaphore_wait(barrier, times + chans - 2)
    send_times(0)

    def more(b, _):
        first(b)
        send_times(b)
        return 0
    lax.fori_loop(1, batch, more, 0)

    def second(b, _):
        load(2, b).wait()

        def block(k, _):
            at = rows(k)
            opened = 1.0 + jnp.tanh(0.5 * gate[b, at, :].astype(jnp.float32))
            dec[b, at, :] = jnp.exp2(-dec[b, at, :]) * opened
            run[b, at, :] = jnp.dot(tri_ref[...], split(run[b, at, :]),
                                    preferred_element_type=jnp.float32)
            return 0
        lax.fori_loop(0, blocks, block, 0)
        return 0
    lax.fori_loop(0, batch, second, 0)

    def third(b, _):
        def arrive(peer, state):
            time_arrival(b, peer).wait_recv()
            return theirs[b, peer, 0:1, :] * state + theirs[b, peer, 1:2, :]
        state = lax.fori_loop(0, t, arrive, jnp.zeros((1, width), jnp.float32))

        def block(k, state):
            at = rows(k)
            gated = dec[b, at, :] * (run[b, at, :] + state)
            run[b, at, :] = gated
            squares = gated * gated
            folded = squares[:, :LANES]
            for lane in range(LANES, width, LANES):
                folded = folded + squares[:, lane:lane + LANES]
            power[b, pl.ds(k, 1), :] = lax.dot_general(
                jnp.ones((8, LANES), jnp.float32), folded, (((1,), (1,)), ((), ())),
                precision=lax.Precision.HIGHEST, preferred_element_type=jnp.float32)[0:1]
            return keeps[b, k] * (state + sums[b, k])
        lax.fori_loop(0, blocks, block, state)
        for step in range(1, chans):
            chan_copy(b, step).start()
        return 0
    lax.fori_loop(0, batch, third, 0)

    def fourth(b, _):
        mean = power[b]
        for step in range(1, chans):
            chan_copy(b, step).wait_recv()
            mean = mean + powers[b, step - 1]
        mean = mean * (scale * scale / (width * chans))
        factor = scale * lax.rsqrt(mean + 1e-6)
        gain = gain_ref[...]
        for k in range(blocks):
            at = pl.ds(k * BLOCK, BLOCK)
            tall = jnp.transpose(jnp.broadcast_to(factor[k:k + 1, :], (LANES, BLOCK)))
            for lane in range(0, width, LANES):
                cut = pl.ds(lane, LANES)
                outb[b, at, cut] = (run[b, at, cut] * tall * gain[:, lane:lane + LANES]).astype(outb.dtype)
        store(b).start()
        return 0
    lax.fori_loop(0, batch, fourth, 0)

    def finish(b, _):
        def sent(peer, _):
            time_copy(b, peer).wait_send()
            return 0
        lax.fori_loop(t + 1, times, sent, 0)
        for step in range(1, chans):
            chan_copy(b, step).wait_send()
        store(b).wait()
        return 0
    lax.fori_loop(0, batch, finish, 0)


def shards(decay_rate, drive_in, gate_in, norm_gain):
    times, chans = lax.axis_size("time"), lax.axis_size("chan")
    batch, length, width = decay_rate.shape
    blocks = length // BLOCK
    lower = jnp.tril(jnp.ones((BLOCK, BLOCK), jnp.bfloat16))
    any_space = pl.BlockSpec(memory_space=pl.ANY)
    vmem = pl.BlockSpec(memory_space=pltpu.VMEM)
    dma = pltpu.SemaphoreType.DMA
    f32 = jnp.float32
    return pl.pallas_call(
        functools.partial(kernel, times, chans),
        out_shape=jax.ShapeDtypeStruct(decay_rate.shape, jnp.bfloat16),
        in_specs=[any_space] * 3 + [vmem] * 2,
        out_specs=any_space,
        scratch_shapes=[
            pltpu.VMEM((batch, length, width), f32),
            pltpu.VMEM((batch, length, width), drive_in.dtype),
            pltpu.VMEM((batch, length, width), gate_in.dtype),
            pltpu.VMEM((batch, length, width), f32),
            pltpu.VMEM((batch, length, width), jnp.bfloat16),
            pltpu.VMEM((batch, blocks, 1, width), f32),
            pltpu.VMEM((batch, blocks, 1, width), f32),
            pltpu.VMEM((batch, 2, width), f32),
            pltpu.VMEM((batch, times, 2, width), f32),
            pltpu.VMEM((batch, blocks, BLOCK), f32),
            pltpu.VMEM((batch, chans - 1, blocks, BLOCK), f32),
            dma((3, batch)),
            dma((batch,)),
            dma((batch, times)),
            dma((batch, times)),
            dma((batch, chans - 1)),
            dma((batch, chans - 1)),
        ],
        compiler_params=pltpu.CompilerParams(
            collective_id=0, has_side_effects=True, vmem_limit_bytes=60 * 2 ** 20),
    )(decay_rate, drive_in, gate_in, norm_gain.reshape(1, width), jnp.concatenate([lower, lower], axis=1))


def solution(mesh):
    placed = (P(None, "time", "chan"), P(None, "time", "chan"), P(None, "time", "chan"), P("chan"))
    return jax.shard_map(
        shards, mesh=mesh, in_specs=placed, out_specs=P(None, "time", "chan"), check_vma=False
    )
```

time: 256 us -> 29.7 us (0.12); the launches traced: 253 us -> 29.5 us
  local copies, waits for them, and re-layouts: 163 us -> 4.72 us
  other arithmetic: 57.2 us -> 0.65 us
  blocking collectives: 32.1 us -> 0 us
  Pallas kernels: 0 us -> 24.1 us
    slice x53 -> x0, local copies, waits for them, and re-layouts: 132 us -> none  [the longest x52 131 us: shards(): forward = lax.associative_scan(join_pair, (keep, started), axis=1)[1]]
    pad x16 -> x0, local copies, waits for them, and re-layouts: 26 us -> none  [shards(): forward = lax.associative_scan(join_pair, (keep, started), axis=1)[1]]
    pallas_call x0 -> x1, Pallas kernels: none -> 24.1 us  [shards(): pl.pallas_call(functools.partial(kernel, times, chans), out_shape=jax.Sha...]
    all_gather x2 -> x0, blocking collectives: 20 us -> none  [entering(): pieces = jax.tree.map(lambda part: lax.all_gather(part, axis), value)]
    psum x1 -> x0, blocking collectives: 12.1 us -> none  [shards(): lax.psum(jnp.sum(gated * gated, axis=-1, keepdims=True), 'chan')]
    mul x8 -> x0, other arithmetic: 11.9 us -> none  [the longest x7 11.8 us: join_pair(): return (earlier[0] * later[0], later[0] * earlier[1] + later[1])]
    another operation x4 -> x0, other arithmetic: 11.7 us -> none
    add x18 -> x0, other arithmetic: 10.4 us -> none  [the longest x9 6.21 us: join_pair(): return (earlier[0] * later[0], later[0] * earlier[1] + later[1])]
where the time goes in v1:
time: 29.7 us; the launch traced here: 29.5 us
  Pallas kernels  24.1 us (81%)
  local copies, waits for them, and re-layouts  4.72 us (16%)
  other arithmetic  0.65 us (2%)
    pallas_call x1, Pallas kernels, shards(): pl.pallas_call(functools.partial(kernel, times, chans), out_shape=jax.Sha...  24.1 us
    unnamed x1, local copies, waits for them, and re-layouts  3.46 us
    reshape x1, local copies, waits for them, and re-layouts, shards(): norm_gain.reshape(1, width)  1.26 us
    concatenate x1, other arithmetic, shards(): jnp.concatenate([lower, lower], axis=1)  0.63 us

profile of v1, /device:TPU:0, one launch (start us, length us, event | category | flops | bytes accessed | tf_op | source)
XLA Modules:
  0.0 29.5 jit_solution(7962857908427626695)
XLA Ops:
  0.0 1.3 %reshape.3.gain_ref = f32[1,640]{1,0:T(1,128)} reshape(f32[640]{0:T(1024)} %param.7) | data formatting | bytes 5120 | tf_op jit(solution)/shard_map/reshape | solution.py:215
  1.3 0.6 %pad_maximum_fusion.tri_ref = bf16[128,256]{1,0:T(8,128)(2,1)} fusion(bf16[128,128]{1,0:T(8,128)(2,1)S(1)} %fusion), kind=kLoop, calls=%fused_computation | loop fusion | flops 131072 | bytes 98304 | tf_op jit(solution)/shard_map/concatenate | solution.py:215
  1.9 24.1 %shard_map.46 = bf16[4,512,640]{2,1,0:T(8,128)(2,1)} custom-call(f32[4,512,640]{2,1,0:T(8,128)} %dec_hbm.1, bf16[4,512,640]{2,1,0:T(8,128)(2,1)} %drv_hbm.1, bf16[4,512,640]{2,1,0:T(8,128)(2,1)} %gate_hbm.1, f32[1,640]{1,0:T(1,128)} %reshape.3.gain_ref, bf16[128,256]{1,0:T(8,128)(2,1)} %pad_maximum_fusion.tri_ref), custom_call_target="tpu_custom_call" | custom-call | tf_op jit(solution)/shard_map/pallas_call | solution.py:189
  26.0 3.5 %copy.6 = bf16[4,512,640]{2,1,0:T(8,128)(2,1)} copy(bf16[4,512,640]{2,1,0:T(8,128)(2,1)} %shard_map.46) | data formatting | bytes 5242880
  (1 shorter events, 0.0 us)

commit v2 on v1

--- a/solution.py
+++ b/solution.py
@@ -19,9 +19,9 @@
     return jnp.concatenate([hi, lo], axis=0)
 
 
-def kernel(times, chans, dec_hbm, drv_hbm, gate_hbm, gain_ref, tri_ref, out_hbm,
-           dec, drv, gate, run, outb, keeps, sums, mine, theirs, power, powers,
-           in_sem, out_sem, t_send, t_recv, c_send, c_recv):
+def kernel(times, chans, dec_hbm, drv_hbm, gate_hbm, gain_ref, outb,
+           tri_ref, dec, drv, gate, run, keeps, sums, mine, theirs, power, powers,
+           in_sem, t_send, t_recv, c_send, c_recv):
     batch, length, width = dec.shape
     blocks = length // BLOCK
     total = length * times
@@ -33,9 +33,6 @@
 
     def load(i, b):
         return pltpu.make_async_copy(places[i][0].at[b], places[i][1].at[b], in_sem.at[i, b])
-
-    def store(b):
-        return pltpu.make_async_copy(outb.at[b], out_hbm.at[b], out_sem.at[b])
 
     def time_copy(b, peer):
         return pltpu.make_async_remote_copy(
@@ -66,6 +63,12 @@
     for step in range(1, chans):
         pl.semaphore_signal(barrier, inc=1, device_id={"chan": lax.rem(c + step, chans)},
                             device_id_type=MESH)
+
+    below = lax.broadcasted_iota(jnp.int32, (BLOCK, BLOCK), 0) >= lax.broadcasted_iota(
+        jnp.int32, (BLOCK, BLOCK), 1)
+    lower = jnp.where(below, 1.0, 0.0).astype(jnp.bfloat16)
+    tri_ref[:, :BLOCK] = lower
+    tri_ref[:, BLOCK:] = lower
 
     def rows(k):
         return pl.ds(pl.multiple_of(k * BLOCK, BLOCK), BLOCK)
@@ -154,14 +157,13 @@
             mean = mean + powers[b, step - 1]
         mean = mean * (scale * scale / (width * chans))
         factor = scale * lax.rsqrt(mean + 1e-6)
-        gain = gain_ref[...]
+        gain = gain_ref[...].reshape(1, width)
         for k in range(blocks):
             at = pl.ds(k * BLOCK, BLOCK)
             tall = jnp.transpose(jnp.broadcast_to(factor[k:k + 1, :], (LANES, BLOCK)))
             for lane in range(0, width, LANES):
                 cut = pl.ds(lane, LANES)
                 outb[b, at, cut] = (run[b, at, cut] * tall * gain[:, lane:lane + LANES]).astype(outb.dtype)
-        store(b).start()
         return 0
     lax.fori_loop(0, batch, fourth, 0)
 
@@ -172,7 +174,6 @@
         lax.fori_loop(t + 1, times, sent, 0)
         for step in range(1, chans):
             chan_copy(b, step).wait_send()
-        store(b).wait()
         return 0
     lax.fori_loop(0, batch, finish, 0)
 
@@ -181,22 +182,21 @@
     times, chans = lax.axis_size("time"), lax.axis_size("chan")
     batch, length, width = decay_rate.shape
     blocks = length // BLOCK
-    lower = jnp.tril(jnp.ones((BLOCK, BLOCK), jnp.bfloat16))
     any_space = pl.BlockSpec(memory_space=pl.ANY)
     vmem = pl.BlockSpec(memory_space=pltpu.VMEM)
     dma = pltpu.SemaphoreType.DMA
     f32 = jnp.float32
     return pl.pallas_call(
         functools.partial(kernel, times, chans),
-        out_shape=jax.ShapeDtypeStruct(decay_rate.shape, jnp.bfloat16),
-        in_specs=[any_space] * 3 + [vmem] * 2,
-        out_specs=any_space,
+        out_shape=pltpu.VMEM(decay_rate.shape, jnp.bfloat16),
+        in_specs=[any_space] * 3 + [vmem],
+        out_specs=vmem,
         scratch_shapes=[
+            pltpu.VMEM((BLOCK, 2 * BLOCK), jnp.bfloat16),
             pltpu.VMEM((batch, length, width), f32),
             pltpu.VMEM((batch, length, width), drive_in.dtype),
             pltpu.VMEM((batch, length, width), gate_in.dtype),
             pltpu.VMEM((batch, length, width), f32),
-            pltpu.VMEM((batch, length, width), jnp.bfloat16),
             pltpu.VMEM((batch, blocks, 1, width), f32),
             pltpu.VMEM((batch, blocks, 1, width), f32),
             pltpu.VMEM((batch, 2, width), f32),
@@ -204,15 +204,14 @@
             pltpu.VMEM((batch, blocks, BLOCK), f32),
             pltpu.VMEM((batch, chans - 1, blocks, BLOCK), f32),
             dma((3, batch)),
-            dma((batch,)),
             dma((batch, times)),
             dma((batch, times)),
             dma((batch, chans - 1)),
             dma((batch, chans - 1)),
         ],
         compiler_params=pltpu.CompilerParams(
-            collective_id=0, has_side_effects=True, vmem_limit_bytes=60 * 2 ** 20),
-    )(decay_rate, drive_in, gate_in, norm_gain.reshape(1, width), jnp.concatenate([lower, lower], axis=1))
+            collective_id=0, has_side_effects=True, vmem_limit_bytes=58 * 2 ** 20),
+    )(decay_rate, drive_in, gate_in, norm_gain)
 
 
 def solution(mesh):

time: 29.7 us -> 24.9 us (0.84)
  local copies, waits for them, and re-layouts: 4.72 us -> 1.49 us
  Pallas kernels: 24.1 us -> 23.2 us
  other arithmetic: 0.65 us -> 0 us
    unnamed x1, local copies, waits for them, and re-layouts: 3.46 us -> 1.49 us
    reshape x1 -> x0, local copies, waits for them, and re-layouts: 1.26 us -> none  [shards(): norm_gain.reshape(1, width)]
    pallas_call x1, Pallas kernels: 24.1 us -> 23.2 us  [shards(): pl.pallas_call(functools.partial(kernel, times, chans), out_shape=pltpu.V...]
    concatenate x1 -> x0, other arithmetic: 0.63 us -> none  [shards(): jnp.concatenate([lower, lower], axis=1)]
where the time goes in v2:
time: 24.9 us; the launch traced here: 24.7 us
  Pallas kernels  23.2 us (93%)
  local copies, waits for them, and re-layouts  1.49 us (6%)
    pallas_call x1, Pallas kernels, shards(): pl.pallas_call(functools.partial(kernel, times, chans), out_shape=pltpu.V...  23.2 us
    unnamed x1, local copies, waits for them, and re-layouts  1.49 us

profile of v2, /device:TPU:0, one launch (start us, length us, event | category | flops | bytes accessed | tf_op | source)
XLA Modules:
  0.0 24.7 jit_solution(3024606172917516047)
XLA Ops:
  0.0 23.2 %shard_map.46 = bf16[4,512,640]{2,1,0:T(8,128)(2,1)S(1)} custom-call(f32[4,512,640]{2,1,0:T(8,128)} %dec_hbm.1, bf16[4,512,640]{2,1,0:T(8,128)(2,1)} %drv_hbm.1, bf16[4,512,640]{2,1,0:T(8,128)(2,1)} %gate_hbm.1, f32[640]{0:T(1024)} %gain_ref.1), custom_call_target="tpu_custom_call" | custom-call | tf_op jit(solution)/shard_map/pallas_call | solution.py:189
  23.2 1.5 %copy.6 = bf16[4,512,640]{2,1,0:T(8,128)(2,1)} copy(bf16[4,512,640]{2,1,0:T(8,128)(2,1)S(1)} %shard_map.46) | data formatting | bytes 5242880

commit v3 on v2

--- a/solution.py
+++ b/solution.py
@@ -10,6 +10,7 @@
 
 BLOCK = 128
 LANES = 128
+PIECE = 64
 MESH = pl.DeviceIdType.MESH
 
 
@@ -19,9 +20,9 @@
     return jnp.concatenate([hi, lo], axis=0)
 
 
-def kernel(times, chans, dec_hbm, drv_hbm, gate_hbm, gain_ref, outb,
-           tri_ref, dec, drv, gate, run, keeps, sums, mine, theirs, power, powers,
-           in_sem, t_send, t_recv, c_send, c_recv):
+def kernel(times, chans, dec_hbm, drv_hbm, gate_hbm, gain_hbm, outb,
+           gain_ref, tri_ref, dec, drv, gate, run, keeps, sums, mine, theirs, folds, power, powers,
+           in_sem, head_sem, gain_sem, t_send, t_recv, c_send, c_recv):
     batch, length, width = dec.shape
     blocks = length // BLOCK
     total = length * times
@@ -50,11 +51,17 @@
             recv_sem=c_recv.at[b, step - 1], device_id={"chan": lax.rem(c + step, chans)},
             device_id_type=MESH)
 
-    for b in range(batch):
-        load(0, b).start()
-        load(1, b).start()
-    for b in range(batch):
-        load(2, b).start()
+    def head(i, k):
+        at = pl.ds(k * BLOCK, BLOCK)
+        return pltpu.make_async_copy(
+            places[i][0].at[0, at], places[i][1].at[0, at], head_sem.at[i, k])
+
+    for k in range(blocks):
+        head(0, k).start()
+        head(1, k).start()
+    if batch > 1:
+        load(0, 1).start()
+        load(1, 1).start()
 
     barrier = pltpu.get_barrier_semaphore()
     for step in range(1, times):
@@ -73,11 +80,15 @@
     def rows(k):
         return pl.ds(pl.multiple_of(k * BLOCK, BLOCK), BLOCK)
 
-    def first(b):
-        load(0, b).wait()
-        load(1, b).wait()
+    def first(b, early):
+        if not early:
+            load(0, b).wait()
+            load(1, b).wait()
 
         def block(k, carried):
+            if early:
+                head(0, k).wait()
+                head(1, k).wait()
             kept, state = carried
             at = rows(k)
             so_far = rate * jnp.dot(tri_ref[...], split(dec[b, at, :]),
@@ -102,31 +113,41 @@
             return 0
         lax.fori_loop(t + 1, times, send, 0)
 
-    first(0)
+    for b in range(2, batch):
+        load(0, b).start()
+        load(1, b).start()
+    first(0, True)
+    for b in range(batch):
+        load(2, b).start()
+    gain_copy = pltpu.make_async_copy(gain_hbm, gain_ref, gain_sem)
+    gain_copy.start()
     pl.semaphore_wait(barrier, times + chans - 2)
     send_times(0)
 
     def more(b, _):
-        first(b)
+        first(b, False)
         send_times(b)
         return 0
     lax.fori_loop(1, batch, more, 0)
 
-    def second(b, _):
+    def second(b):
         load(2, b).wait()
+
+        def opening(k, _):
+            at = pl.ds(pl.multiple_of(k * PIECE, PIECE), PIECE)
+            opened = 1.0 + jnp.tanh(0.5 * gate[b, at, :].astype(jnp.float32))
+            dec[b, at, :] = jnp.exp2(-dec[b, at, :]) * opened
+            return 0
+        lax.fori_loop(0, length // PIECE, opening, 0)
 
         def block(k, _):
             at = rows(k)
-            opened = 1.0 + jnp.tanh(0.5 * gate[b, at, :].astype(jnp.float32))
-            dec[b, at, :] = jnp.exp2(-dec[b, at, :]) * opened
             run[b, at, :] = jnp.dot(tri_ref[...], split(run[b, at, :]),
                                     preferred_element_type=jnp.float32)
             return 0
         lax.fori_loop(0, blocks, block, 0)
-        return 0
-    lax.fori_loop(0, batch, second, 0)
-
-    def third(b, _):
+
+    def third(b):
         def arrive(peer, state):
             time_arrival(b, peer).wait_recv()
             return theirs[b, peer, 0:1, :] * state + theirs[b, peer, 1:2, :]
@@ -140,15 +161,26 @@
             folded = squares[:, :LANES]
             for lane in range(LANES, width, LANES):
                 folded = folded + squares[:, lane:lane + LANES]
-            power[b, pl.ds(k, 1), :] = lax.dot_general(
-                jnp.ones((8, LANES), jnp.float32), folded, (((1,), (1,)), ((), ())),
-                precision=lax.Precision.HIGHEST, preferred_element_type=jnp.float32)[0:1]
+            hi = folded.astype(jnp.bfloat16)
+            folds[at, :LANES] = hi
+            folds[at, LANES:] = (folded - hi.astype(jnp.float32)).astype(jnp.bfloat16)
             return keeps[b, k] * (state + sums[b, k])
         lax.fori_loop(0, blocks, block, state)
+        power[b] = lax.dot_general(
+            jnp.ones((8, 2 * LANES), jnp.bfloat16), folds[...], (((1,), (1,)), ((), ())),
+            preferred_element_type=jnp.float32)[0:1]
         for step in range(1, chans):
             chan_copy(b, step).start()
-        return 0
-    lax.fori_loop(0, batch, third, 0)
+
+    second(0)
+
+    def middle(b, _):
+        second(b)
+        third(b - 1)
+        return 0
+    lax.fori_loop(1, batch, middle, 0)
+    third(batch - 1)
+    gain_copy.wait()
 
     def fourth(b, _):
         mean = power[b]
@@ -160,7 +192,7 @@
         gain = gain_ref[...].reshape(1, width)
         for k in range(blocks):
             at = pl.ds(k * BLOCK, BLOCK)
-            tall = jnp.transpose(jnp.broadcast_to(factor[k:k + 1, :], (LANES, BLOCK)))
+            tall = jnp.transpose(jnp.broadcast_to(factor[:, k * BLOCK:(k + 1) * BLOCK], (LANES, BLOCK)))
             for lane in range(0, width, LANES):
                 cut = pl.ds(lane, LANES)
                 outb[b, at, cut] = (run[b, at, cut] * tall * gain[:, lane:lane + LANES]).astype(outb.dtype)
@@ -189,9 +221,10 @@
     return pl.pallas_call(
         functools.partial(kernel, times, chans),
         out_shape=pltpu.VMEM(decay_rate.shape, jnp.bfloat16),
-        in_specs=[any_space] * 3 + [vmem],
+        in_specs=[any_space] * 4,
         out_specs=vmem,
         scratch_shapes=[
+            pltpu.VMEM((width,), f32),
             pltpu.VMEM((BLOCK, 2 * BLOCK), jnp.bfloat16),
             pltpu.VMEM((batch, length, width), f32),
             pltpu.VMEM((batch, length, width), drive_in.dtype),
@@ -201,9 +234,12 @@
             pltpu.VMEM((batch, blocks, 1, width), f32),
             pltpu.VMEM((batch, 2, width), f32),
             pltpu.VMEM((batch, times, 2, width), f32),
-            pltpu.VMEM((batch, blocks, BLOCK), f32),
-            pltpu.VMEM((batch, chans - 1, blocks, BLOCK), f32),
+            pltpu.VMEM((length, 2 * LANES), jnp.bfloat16),
+            pltpu.VMEM((batch, 1, length), f32),
+            pltpu.VMEM((batch, chans - 1, 1, length), f32),
             dma((3, batch)),
+            dma((2, blocks)),
+            dma,
             dma((batch, times)),
             dma((batch, times)),
             dma((batch, chans - 1)),

time: 24.9 us -> 22.5 us (0.904)
  Pallas kernels: 23.2 us -> 20.9 us
    pallas_call x1, Pallas kernels: 23.2 us -> 20.9 us  [shards(): pl.pallas_call(functools.partial(kernel, times, chans), out_shape=pltpu.V...]
where the time goes in v3:
time: 22.5 us; the launch traced here: 22.4 us
  Pallas kernels  20.9 us (93%)
  local copies, waits for them, and re-layouts  1.49 us (7%)
    pallas_call x1, Pallas kernels, shards(): pl.pallas_call(functools.partial(kernel, times, chans), out_shape=pltpu.V...  20.9 us
    unnamed x1, local copies, waits for them, and re-layouts  1.49 us

profile of v3, /device:TPU:0, one launch (start us, length us, event | category | flops | bytes accessed | tf_op | source)
XLA Modules:
  0.0 22.4 jit_solution(13631120245870238006)
XLA Ops:
  0.0 20.9 %shard_map.46 = bf16[4,512,640]{2,1,0:T(8,128)(2,1)S(1)} custom-call(f32[4,512,640]{2,1,0:T(8,128)} %dec_hbm.1, bf16[4,512,640]{2,1,0:T(8,128)(2,1)} %drv_hbm.1, bf16[4,512,640]{2,1,0:T(8,128)(2,1)} %gate_hbm.1, f32[640]{0:T(1024)} %gain_hbm.1), custom_call_target="tpu_custom_call" | custom-call | tf_op jit(solution)/shard_map/pallas_call | solution.py:221
  20.9 1.5 %copy.6 = bf16[4,512,640]{2,1,0:T(8,128)(2,1)} copy(bf16[4,512,640]{2,1,0:T(8,128)(2,1)S(1)} %shard_map.46) | data formatting | bytes 5242880

commit v4 on v3

--- a/solution.py
+++ b/solution.py
@@ -103,7 +103,7 @@
             return kept * keep, keep * (state + gained)
 
         kept, state = lax.fori_loop(
-            0, blocks, block, (jnp.ones((1, width), jnp.float32), jnp.zeros((1, width), jnp.float32)))
+            0, blocks, block, (jnp.ones((1, width), jnp.float32), jnp.zeros((1, width), jnp.float32)), unroll=2)
         mine[b, 0:1, :] = kept
         mine[b, 1:2, :] = state
 
@@ -145,7 +145,7 @@
             run[b, at, :] = jnp.dot(tri_ref[...], split(run[b, at, :]),
                                     preferred_element_type=jnp.float32)
             return 0
-        lax.fori_loop(0, blocks, block, 0)
+        lax.fori_loop(0, blocks, block, 0, unroll=2)
 
     def third(b):
         def arrive(peer, state):

time: 22.5 us -> 22.6 us (level)
  no operation moved by 1% of the time
where the time goes in v4:
time: 22.6 us; the launch traced here: 22.5 us
  Pallas kernels  21 us (93%)
  local copies, waits for them, and re-layouts  1.49 us (7%)
    pallas_call x1, Pallas kernels, shards(): pl.pallas_call(functools.partial(kernel, times, chans), out_shape=pltpu.V...  21 us
    unnamed x1, local copies, waits for them, and re-layouts  1.49 us

profile of v4, /device:TPU:0, one launch (start us, length us, event | category | flops | bytes accessed | tf_op | source)
XLA Modules:
  0.0 22.5 jit_solution(6219079281204213824)
XLA Ops:
  0.0 21.0 %shard_map.46 = bf16[4,512,640]{2,1,0:T(8,128)(2,1)S(1)} custom-call(f32[4,512,640]{2,1,0:T(8,128)} %dec_hbm.1, bf16[4,512,640]{2,1,0:T(8,128)(2,1)} %drv_hbm.1, bf16[4,512,640]{2,1,0:T(8,128)(2,1)} %gate_hbm.1, f32[640]{0:T(1024)} %gain_hbm.1), custom_call_target="tpu_custom_call" | custom-call | tf_op jit(solution)/shard_map/pallas_call | solution.py:221
  21.0 1.5 %copy.6 = bf16[4,512,640]{2,1,0:T(8,128)(2,1)} copy(bf16[4,512,640]{2,1,0:T(8,128)(2,1)S(1)} %shard_map.46) | data formatting | bytes 5242880
